TPU v7x, 32 devices: a whole 2x2x4 slice. The times are simulated.
32 devices in a mesh: row: 4 (over z), col: 8 (over y, x, core).
Axes of the slice: x: 2, y: 2, z: 4, core: 2. Of those that a mesh axis runs over, the one named last changes fastest.
Arguments:
- minus_gradient: float32 [6, 16384], P(None, ('row', 'col')), may hold values from -10 to 10
- diag_blocks: float32 [36, 16384], P(None, ('row', 'col')), may hold values from -1000 to 1000, as said below
- hess_blocks: float32 [4, 8, 36, 4096], P('row', 'col'), may hold values from -40 to 40, as said below
- block_rows: int32 [4, 8, 4096], P('row', 'col'), may hold values from 0 to 2047
- block_cols: int32 [4, 8, 4096], P('row', 'col'), may hold values from 0 to 4095
- block_counts: int32 [4, 8], P('row', 'col'), may hold values from 0 to 4096, as said below
Outputs:
- pose_update: float32 [6, 16384], P(None, ('row', 'col'))
- residual: float32 [6, 16384], P(None, ('row', 'col'))
Inputs may be any that keep to these rules, and one draw needn't show every extreme that they name: `hess_blocks`: the live blocks of all tiles together with diag_blocks form a symmetric positive definite matrix; no live block lies on the diagonal; the slots after the live ones hold arbitrary entries. `diag_blocks`: each 6x6 block is symmetric positive definite. The live slots of a tile are its first block_counts slots.
All inputs are finite; a program needn't handle non-finite values.
Results may differ from a plain program's by a relative error of at most 0.0003.
Values sent between devices are 32-bit elements; how exact they have to be, the bound alone decides.
A program may use at most 64 MiB of HBM per device.

v0:
```python
import math

import jax
import jax.numpy as jnp
from jax import lax
from jax.sharding import PartitionSpec as P

ITERS = 3


def factor_blocks(blocks):
    lower_part = {}
    reciprocals = []
    for j in range(6):
        pivot_value = blocks[7 * j]
        for k in range(j):
            pivot_value = pivot_value - lower_part[j, k] * lower_part[j, k]
        reciprocal = 1.0 / jnp.sqrt(pivot_value)
        reciprocals.append(reciprocal)
        for i in range(j + 1, 6):
            entry_value = blocks[6 * i + j]
            for k in range(j):
                entry_value = entry_value - lower_part[i, k] * lower_part[j, k]
            lower_part[i, j] = entry_value * reciprocal
    return (lower_part, reciprocals)


def apply_inverse(lower_part, reciprocals, vector):
    forward = []
    for i in range(6):
        running = vector[i]
        for k in range(i):
            running = running - lower_part[i, k] * forward[k]
        forward.append(running * reciprocals[i])
    backward = [None] * 6
    for i in range(5, -1, -1):
        running = forward[i]
        for k in range(i + 1, 6):
            running = running - lower_part[k, i] * backward[k]
        backward[i] = running * reciprocals[i]
    return jnp.stack(backward)


def diagonal_term(diag_blocks, vector):
    return jnp.sum(diag_blocks.reshape(6, 6, -1) * vector[None], axis=1)


def pick_columns(source, offsets):
    width = source.shape[1]
    low_width = math.gcd(128, width)
    high_width = width // low_width
    table = source.reshape(6 * high_width, low_width)
    slot_count = offsets.shape[0]
    block_size = math.gcd(512, slot_count)
    turns = slot_count // block_size

    def pick_one_block(carry, offset):
        low_part = offset % low_width
        high_part = offset // low_width
        low_onehot = (
            lax.broadcasted_iota(jnp.int32, (low_width, block_size), 0) == low_part[None, :]
        ).astype(jnp.float32)
        spread = jnp.dot(
            table, low_onehot, precision=lax.Precision.HIGHEST, preferred_element_type=jnp.float32
        )
        high_onehot = (
            lax.broadcasted_iota(jnp.int32, (high_width, block_size), 0) == high_part[None, :]
        ).astype(jnp.float32)
        chosen = jnp.sum(spread.reshape(6, high_width, block_size) * high_onehot[None], axis=1)
        return (carry, chosen)

    unused, blocks_out = lax.scan(pick_one_block, None, offsets.reshape(turns, block_size))
    return jnp.transpose(blocks_out, (1, 0, 2)).reshape(6, slot_count)


def add_rows(terms, rows, span_size):
    low_width = math.gcd(128, span_size)
    high_width = span_size // low_width
    slot_count = rows.shape[0]
    block_size = math.gcd(512, slot_count)
    turns = slot_count // block_size
    term_blocks = jnp.transpose(terms.reshape(6, turns, block_size), (1, 0, 2))
    row_blocks = rows.reshape(turns, block_size)

    def add_one_block(carry, inputs):
        term_block, row_block = inputs
        high_onehot = (
            lax.broadcasted_iota(jnp.int32, (high_width, block_size), 0)
            == (row_block // low_width)[None, :]
        ).astype(jnp.float32)
        spread = (term_block[:, None, :] * high_onehot[None]).reshape(6 * high_width, block_size)
        low_onehot = (
            (row_block % low_width)[:, None]
            == lax.broadcasted_iota(jnp.int32, (block_size, low_width), 1)
        ).astype(jnp.float32)
        carry = carry + jnp.dot(
            spread, low_onehot, precision=lax.Precision.HIGHEST, preferred_element_type=jnp.float32
        )
        return (carry, None)

    start_total = jnp.zeros((6 * high_width, low_width), jnp.float32)
    total, unused = lax.scan(add_one_block, start_total, (term_blocks, row_blocks))
    return total.reshape(6, span_size)


def merged_sums(residual, precond, hess_image):
    return lax.psum((jnp.sum(residual * precond), jnp.sum(hess_image * precond)), ("row", "col"))


def on_device(minus_gradient, diag_blocks, hess_blocks, block_rows, block_cols, block_counts):
    pose_dev = minus_gradient.shape[1]
    blocks = hess_blocks.reshape(6, 6, -1)
    local_rows = block_rows.reshape(-1)
    local_cols = block_cols.reshape(-1)
    slot_count = local_rows.shape[0]
    live_mask = jnp.arange(slot_count, dtype=jnp.int32) < block_counts.reshape(())
    span_size = pose_dev * lax.axis_size("row")
    lower_part, reciprocals = factor_blocks(diag_blocks)

    def tile_terms(picked):
        return jnp.sum(blocks * picked[None], axis=1)

    def hessian(vector):
        gathered = lax.all_gather(vector, "col", axis=1, tiled=True)
        picked = pick_columns(gathered, local_cols)
        live_terms = jnp.where(live_mask[None, :], tile_terms(picked), 0.0)
        partial_value = add_rows(live_terms, local_rows, span_size)
        own_term = diagonal_term(diag_blocks, vector)
        summed = lax.psum(partial_value, "row")
        reduced = lax.dynamic_slice_in_dim(summed, lax.axis_index("row") * pose_dev, pose_dev, 1)
        return reduced + own_term

    solution = jnp.zeros_like(minus_gradient)
    residual = minus_gradient
    precond = apply_inverse(lower_part, reciprocals, residual)
    hess_image = hessian(precond)
    rho_now, curv_value = merged_sums(residual, precond, hess_image)
    step_size = rho_now / curv_value
    direction = precond
    along_image = hess_image
    for k in range(ITERS):
        solution = solution + step_size * direction
        residual = residual - step_size * along_image
        if k + 1 < ITERS:
            precond = apply_inverse(lower_part, reciprocals, residual)
            hess_image = hessian(precond)
            rho_next, curv_value = merged_sums(residual, precond, hess_image)
            ratio_next = rho_next / rho_now
            step_size = rho_next / (curv_value - ratio_next * rho_next / step_size)
            direction = precond + ratio_next * direction
            along_image = hess_image + ratio_next * along_image
            rho_now = rho_next
    return (solution, residual)


def solution(mesh):
    placed = (
        P(None, ("row", "col")),
        P(None, ("row", "col")),
        P("row", "col", None, None),
        P("row", "col", None),
        P("row", "col", None),
        P("row", "col"),
    )
    return jax.shard_map(
        on_device,
        mesh=mesh,
        in_specs=placed,
        out_specs=(P(None, ("row", "col")), P(None, ("row", "col"))),
        check_vma=False,
    )
```

profile of v0, /device:TPU:0, one launch (start us, length us, event | category | flops | bytes accessed | tf_op | source)
XLA Modules:
  0.0 246.5 jit_solution(5160269623161957242)
XLA Ops:
  0.6 1.1 subtract_multiply_fusion.21
  1.7 0.7 copy-done.2
  2.6 10.7 %all_gather.9 = f32[6,4096]{1,0:T(8,128)S(1)} all-gather(f32[6,512]{1,0:T(8,128)S(1)} %stack.6), channel_id=1, replica_groups=mesh['row'=4,'col'=8] {'col'}, dimensions={1}, use_global_device_ids=true | all-gather | bytes 110592 | tf_op jit(solution)/shard_map/all_gather | solution.py:124
  14.0 0.7 reduce.7
  14.7 3.9 %while.75 = (s32[]{:T(128)}, f32[8,6,512]{2,1,0:T(8,128)S(1)}, s32[8,512]{1,0:T(8,128)S(1)}, f32[192,128]{1,0:T(8,128)S(1)}, s32[]{:T(128)}) while((s32[]{:T(128)}, f32[8,6,512]{2,1,0:T(8,128)S(1)}, s32[8,512]{1,0:T(8,128)S(1)}, f32[192,128]{1,0:T(8,128)S(1)}, s32[]{:T(128)}) %tuple.218), condition=%wide.region_4.5_spmd, body=%wide.region_2.4_spmd.sunk | while | flops 151297024 | bytes 1075269 | solution.py:72
  18.7 1.4 reduce
  21.1 0.7 copy-done.4
  21.8 0.7 reduce.8
  22.5 3.9 %while.78 = (s32[]{:T(128)}, f32[96,128]{1,0:T(8,128)S(1)}, f32[8,6,512]{2,1,0:T(8,128)S(1)}, s32[8,512]{1,0:T(8,128)S(1)}, s32[]{:T(128)}, /*index=5*/s32[]{:T(128)}) while((s32[]{:T(128)}, f32[96,128]{1,0:T(8,128)S(1)}, f32[8,6,512]{2,1,0:T(8,128)S(1)}, s32[8,512]{1,0:T(8,128)S(1)}, s32[]{:T(128)}, /*index=5*/s32[]{:T(128)}) %tuple.221), condition=%wide.region_7.8_spmd.clone, body=%wide.region_6.7_spmd.clone.sunk | while | flops 75666432 | bytes 608343 | solution.py:102
  26.4 19.9 %psum.64 = f32[6,2048]{1,0:T(8,128)S(1)} all-reduce(f32[6,2048]{1,0:T(8,128)S(1)} %reshape.316), channel_id=1, replica_groups=mesh['row'=4,'col'=8] {'row'}, use_global_device_ids=true, to_apply=%region_8.9 | all-reduce | flops 12288 | bytes 98304 | tf_op jit(solution)/shard_map/psum | solution.py:129
  47.0 37.8 %all-reduce.2 = (f32[]{:T(128)}, f32[]{:T(128)}) all-reduce(f32[]{:T(128)} %get-tuple-element.394, f32[]{:T(128)} %get-tuple-element.393), channel_id=1, replica_groups=mesh['row'=4,'col'=8] {'row','col'}, use_global_device_ids=true, to_apply=%region_1.2 | all-reduce | flops 2 | bytes 16 | tf_op jit(solution)/shard_map/psum | solution.py:107
  86.3 10.2 %all_gather.10 = f32[6,4096]{1,0:T(8,128)S(1)} all-gather(f32[6,512]{1,0:T(8,128)S(1)} %stack.7), channel_id=1, replica_groups=mesh['row'=4,'col'=8] {'col'}, dimensions={1}, use_global_device_ids=true | all-gather | bytes 110592 | tf_op jit(solution)/shard_map/all_gather | solution.py:124
  96.5 3.9 %while.76 = (s32[]{:T(128)}, f32[8,6,512]{2,1,0:T(8,128)S(1)}, s32[8,512]{1,0:T(8,128)S(1)}, f32[192,128]{1,0:T(8,128)S(1)}, s32[]{:T(128)}) while((s32[]{:T(128)}, f32[8,6,512]{2,1,0:T(8,128)S(1)}, s32[8,512]{1,0:T(8,128)S(1)}, f32[192,128]{1,0:T(8,128)S(1)}, s32[]{:T(128)}) %tuple.236), condition=%wide.region_16.17_spmd, body=%wide.region_14.16_spmd.sunk | while | flops 151297024 | bytes 1075269 | solution.py:72
  100.8 3.9 %while.79 = (s32[]{:T(128)}, f32[96,128]{1,0:T(8,128)S(1)}, f32[8,6,512]{2,1,0:T(8,128)S(1)}, s32[8,512]{1,0:T(8,128)S(1)}, s32[]{:T(128)}, /*index=5*/s32[]{:T(128)}) while((s32[]{:T(128)}, f32[96,128]{1,0:T(8,128)S(1)}, f32[8,6,512]{2,1,0:T(8,128)S(1)}, s32[8,512]{1,0:T(8,128)S(1)}, s32[]{:T(128)}, ...), condition=%wide.region_19.20_spmd.clone, body=%wide.region_18.19_spmd.clone.sunk | while | flops 75666432 | bytes 608343 | solution.py:102
  104.7 18.5 %psum.67 = f32[6,2048]{1,0:T(8,128)S(1)} all-reduce(f32[6,2048]{1,0:T(8,128)S(1)} %reshape.319), channel_id=1, replica_groups=mesh['row'=4,'col'=8] {'row'}, use_global_device_ids=true, to_apply=%region_20.21 | all-reduce | flops 12288 | bytes 98304 | tf_op jit(solution)/shard_map/psum | solution.py:129
  123.2 0.7 multiply_reduce_fusion.11
  123.9 37.8 %all-reduce.1 = (f32[]{:T(128)}, f32[]{:T(128)}) all-reduce(f32[]{:T(128)} %get-tuple-element.392, f32[]{:T(128)} %get-tuple-element.391), channel_id=1, replica_groups=mesh['row'=4,'col'=8] {'row','col'}, use_global_device_ids=true, to_apply=%region_13.14 | all-reduce | flops 2 | bytes 16 | tf_op jit(solution)/shard_map/psum | solution.py:107
  166.4 10.2 %all_gather.11 = f32[6,4096]{1,0:T(8,128)S(1)} all-gather(f32[6,512]{1,0:T(8,128)S(1)} %stack.8), channel_id=1, replica_groups=mesh['row'=4,'col'=8] {'col'}, dimensions={1}, use_global_device_ids=true | all-gather | bytes 110592 | tf_op jit(solution)/shard_map/all_gather | solution.py:124
  176.7 3.9 %while.77 = (s32[]{:T(128)}, f32[8,6,512]{2,1,0:T(8,128)S(1)}, s32[8,512]{1,0:T(8,128)S(1)}, f32[192,128]{1,0:T(8,128)S(1)}, s32[]{:T(128)}) while((s32[]{:T(128)}, f32[8,6,512]{2,1,0:T(8,128)S(1)}, s32[8,512]{1,0:T(8,128)S(1)}, f32[192,128]{1,0:T(8,128)S(1)}, s32[]{:T(128)}) %tuple.237), condition=%wide.region_28.29_spmd, body=%wide.region_26.28_spmd.sunk | while | flops 151297024 | bytes 1075269 | solution.py:72
  181.0 3.9 %while.80 = (s32[]{:T(128)}, f32[96,128]{1,0:T(8,128)S(1)}, f32[8,6,512]{2,1,0:T(8,128)S(1)}, s32[8,512]{1,0:T(8,128)S(1)}, s32[]{:T(128)}, /*index=5*/s32[]{:T(128)}) while((s32[]{:T(128)}, f32[96,128]{1,0:T(8,128)S(1)}, f32[8,6,512]{2,1,0:T(8,128)S(1)}, s32[8,512]{1,0:T(8,128)S(1)}, s32[]{:T(128)}, ...), condition=%wide.region_31.32_spmd.clone, body=%wide.region_30.31_spmd.clone.sunk | while | flops 75666432 | bytes 608343 | solution.py:102
  184.9 18.7 %psum.70 = f32[6,2048]{1,0:T(8,128)S(1)} all-reduce(f32[6,2048]{1,0:T(8,128)S(1)} %reshape.321), channel_id=1, replica_groups=mesh['row'=4,'col'=8] {'row'}, use_global_device_ids=true, to_apply=%region_32.33 | all-reduce | flops 12288 | bytes 98304 | tf_op jit(solution)/shard_map/psum | solution.py:129
  203.6 0.6 multiply_reduce_fusion.9
  204.2 37.7 %all-reduce = (f32[]{:T(128)}, f32[]{:T(128)}) all-reduce(f32[]{:T(128)} %get-tuple-element.390, f32[]{:T(128)} %get-tuple-element.389), channel_id=1, replica_groups=mesh['row'=4,'col'=8] {'row','col'}, use_global_device_ids=true, to_apply=%region_25.26 | all-reduce | flops 2 | bytes 16 | tf_op jit(solution)/shard_map/psum | solution.py:107
  245.9 0.6 multiply_subtract_fusion
  (334 shorter events, 23.5 us)
Async XLA Ops:
  0.6 1.1 copy-start.1
  1.7 0.7 copy-start.2
  13.3 0.7 copy-start.3
  14.7 4.0 %copy-start = (f32[1,1,36,4096]{3,1,2,0:T(1,128)S(1)}, f32[1,1,36,4096]{3,1,2,0:T(1,128)}, u32[]{:S(2)}) copy-start(f32[1,1,36,4096]{3,1,2,0:T(1,128)} %param.20) | copy-start | bytes 1769476
  21.1 0.7 copy-start.4
where the time goes:
time: 248 us; the launch traced here: 247 us
  blocking collectives  201 us (81%)
  matrix products  16.6 us (7%)
  between operations  11.5 us (5%)
  other arithmetic  11.1 us (4%)
  loops' own time  2.93 us (1%)
  local copies, waits for them, and re-layouts  2.92 us (1%)
    psum x3, blocking collectives, merged_sums(): lax.psum((jnp.sum(residual * precond), jnp.sum(hess_image * precond)), ('...  113 us
    psum x3, blocking collectives, hessian(): summed = lax.psum(partial_value, 'row')  57.1 us
    all_gather x3, blocking collectives, hessian(): gathered = lax.all_gather(vector, 'col', axis=1, tiled=True)  31.1 us
    dot_general x24, matrix products, add_one_block(): jnp.dot(spread, low_onehot, precision=lax.Precision.HIGHEST, preferred_el...  8.61 us
    dot_general x24, matrix products, pick_one_block(): jnp.dot(table, low_onehot, precision=lax.Precision.HIGHEST, preferred_ele...  7.99 us

commit v1 on v0

v1 whole, which is shorter than its diff:
```python
import functools

import jax
import jax.numpy as jnp
from jax import lax
from jax.experimental import pallas as pl
from jax.experimental.pallas import tpu as pltpu
from jax.sharding import PartitionSpec as P

ITERS = 3
LANES = 128
SUB = 8
MESH = pl.DeviceIdType.MESH


def xor_index(a, b, n):
    out = 0
    bit = 1
    while bit < n:
        out = out + bit * ((a // bit + b // bit) % 2)
        bit *= 2
    return out


def factor_blocks(entry):
    lower_part = {}
    reciprocals = []
    for j in range(6):
        pivot_value = entry(7 * j)
        for k in range(j):
            pivot_value = pivot_value - lower_part[j, k] * lower_part[j, k]
        reciprocal = 1.0 / jnp.sqrt(pivot_value)
        reciprocals.append(reciprocal)
        for i in range(j + 1, 6):
            entry_value = entry(6 * i + j)
            for k in range(j):
                entry_value = entry_value - lower_part[i, k] * lower_part[j, k]
            lower_part[i, j] = entry_value * reciprocal
    return lower_part, reciprocals


def apply_inverse(lower, recip, vector):
    forward = []
    for i in range(6):
        running = vector[i]
        for k in range(i):
            running = running - lower(i, k) * forward[k]
        forward.append(running * recip(i))
    backward = [None] * 6
    for i in range(5, -1, -1):
        running = forward[i]
        for k in range(i + 1, 6):
            running = running - lower(k, i) * backward[k]
        backward[i] = running * recip(i)
    return backward


def cg_scalars(m):
    rc, pc = [1.0], [1.0]
    xc = [0.0] * ITERS
    rho = m[0]
    for k in range(ITERS):
        hc = [0.0] * (k + 2)
        for i in range(k + 1):
            hc[i] = hc[i] + pc[i]
            hc[i + 1] = hc[i + 1] - pc[i]
        curv = 0.0
        for i in range(k + 1):
            for j in range(k + 2):
                curv = curv + pc[i] * hc[j] * m[i + j]
        step = rho / curv
        for i in range(k + 1):
            xc[i] = xc[i] + step * pc[i]
        rc = [a - step * b for a, b in zip(rc + [0.0], hc)]
        if k + 1 < ITERS:
            rho_next = 0.0
            for i in range(k + 2):
                for j in range(k + 2):
                    rho_next = rho_next + rc[i] * rc[j] * m[i + j]
            ratio = rho_next / rho
            pc = [a + ratio * b for a, b in zip(rc, pc + [0.0])]
            rho = rho_next
    return xc, rc


def kernel(
    nrow, ncol, cnt_ref, g_ref, d_ref, rows_ref, cols_ref, h_any, x_ref, r_ref,
    hbuf, b3, dbuf, lbuf, rv, vv, tab, vrow, tbuf, spread, onehot, part, rbuf, mom, mown,
    hsem, vs_sem, vr_sem, ws_sem, wr_sem, ps_sem, pr_sem, ms_sem, mr_sem,
):
    pose_dev = g_ref.shape[1]
    qn = pose_dev // LANES
    vec = 6 * qn
    nchunk = rows_ref.shape[0]
    stride = nchunk + SUB
    nj = nchunk // SUB
    msg = part.shape[2]
    per = SUB // qn
    pairs = 6 // per
    my_row = lax.axis_index("row")
    my_col = lax.axis_index("col")

    h_copy = pltpu.make_async_copy(h_any, hbuf, hsem)
    h_copy.start()

    barrier = pltpu.get_barrier_semaphore()
    for i in range(1, ncol):
        pl.semaphore_signal(
            barrier, inc=1, device_id=(my_row, xor_index(my_col, i, ncol)), device_id_type=MESH
        )
    for i in range(1, nrow):
        pl.semaphore_signal(
            barrier, inc=1, device_id=(xor_index(my_row, i, nrow), my_col), device_id_type=MESH
        )

    for b in range(6):
        for q in range(qn):
            rv[0, b * qn + q : b * qn + q + 1, :] = g_ref[b : b + 1, q * LANES : (q + 1) * LANES]
    for e in range(0, 36, SUB):
        count = min(SUB, 36 - e)
        for q in range(qn):
            dbuf[pl.ds(e * qn + q, count, stride=qn), :] = d_ref[
                e : e + count, q * LANES : (q + 1) * LANES
            ]

    def diag(e):
        return dbuf[e * qn : (e + 1) * qn, :]

    lower_part, reciprocals = factor_blocks(diag)
    slot_of = {}
    for n, (key, value) in enumerate(list(lower_part.items()) + list(enumerate(reciprocals))):
        slot_of[key] = n
        lbuf[n] = value

    def lower(i, k):
        return lbuf[slot_of[i, k]]

    def recip(i):
        return lbuf[slot_of[i]]

    def precondition(k):
        out = apply_inverse(lower, recip, [rv[k, b * qn : (b + 1) * qn, :] for b in range(6)])
        for b in range(6):
            vv[k, b * qn : (b + 1) * qn, :] = out[b]

    def send_vector(k):
        copies = []
        for i in range(1, ncol):
            copy = pltpu.make_async_remote_copy(
                src_ref=vv.at[k],
                dst_ref=tab.at[k, my_col],
                send_sem=vs_sem.at[k, i],
                recv_sem=vr_sem.at[k, i],
                device_id=(my_row, xor_index(my_col, i, ncol)),
                device_id_type=MESH,
            )
            copy.start()
            copies.append(copy)
        return copies

    def send_rows(k):
        copies = []
        for i in range(1, nrow):
            copy = pltpu.make_async_remote_copy(
                src_ref=vv.at[k],
                dst_ref=vrow.at[my_row],
                send_sem=ws_sem.at[i],
                recv_sem=wr_sem.at[i],
                device_id=(xor_index(my_row, i, nrow), my_col),
                device_id_type=MESH,
            )
            copy.start()
            copies.append(copy)
        return copies

    precondition(0)
    pl.semaphore_wait(barrier, ncol + nrow - 2)
    sends = send_vector(0)

    sub_low = lax.broadcasted_iota(jnp.int32, (LANES, LANES), 0)

    def build_onehot(j, carry):
        low = rows_ref[pl.ds(pl.multiple_of(j * SUB, SUB), SUB), :] % LANES
        for s in range(SUB):
            hot = jnp.where(sub_low == low[s : s + 1, :], 1.0, 0.0).astype(jnp.bfloat16)
            onehot[:, pl.ds(pl.multiple_of((j * SUB + s) * LANES, LANES), LANES)] = hot
        return carry

    lax.fori_loop(0, nj, build_onehot, 0)

    h_copy.wait()
    live_count = cnt_ref[0, 0]
    lane = lax.broadcasted_iota(jnp.int32, (SUB, LANES), 1)
    for c in range(nchunk):
        live = lane + c * LANES < live_count
        for e in range(0, 36, SUB):
            count = min(SUB, 36 - e)
            tile = hbuf[e : e + count, c * LANES : (c + 1) * LANES]
            b3[pl.ds(e * stride + c, count, stride=stride), :] = jnp.where(
                live[:count], tile, 0.0
            )

    sub = lax.broadcasted_iota(jnp.int32, (SUB, LANES), 0)
    sub_q = sub % qn
    sub_b = sub // qn

    def tile_partial(k):
        low = [cols_ref[j * SUB : (j + 1) * SUB, :] % LANES for j in range(nj)]
        high = [cols_ref[j * SUB : (j + 1) * SUB, :] // LANES for j in range(nj)]

        def pick(dev, source, acc):
            acc = list(acc)
            for q in range(qn):
                for j in range(nj):
                    chosen = high[j] == dev * qn + q
                    for b in range(6):
                        row = jnp.broadcast_to(source(b * qn + q), (SUB, LANES))
                        got = jnp.take_along_axis(row, low[j], axis=1)
                        acc[b * nj + j] = jnp.where(chosen, got, acc[b * nj + j])
            return tuple(acc)

        zero = tuple(jnp.zeros((SUB, LANES), jnp.float32) for _ in range(6 * nj))
        acc = pick(my_col, lambda n: vv[k, n : n + 1, :], zero)

        def one_peer(i, acc):
            peer = xor_index(my_col, i, ncol)
            pltpu.make_async_remote_copy(
                src_ref=vv.at[k],
                dst_ref=tab.at[k, peer],
                send_sem=vs_sem.at[k, i],
                recv_sem=vr_sem.at[k, i],
                device_id=(my_row, peer),
                device_id_type=MESH,
            ).wait_recv()
            return pick(peer, lambda n: tab[k, peer, n : n + 1, :], acc)

        acc = lax.fori_loop(1, ncol, one_peer, acc)
        for a in range(6):
            for j in range(nj):
                term = None
                for b in range(6):
                    start = (6 * a + b) * stride + j * SUB
                    product = b3[start : start + SUB, :] * acc[b * nj + j]
                    term = product if term is None else term + product
                tbuf[a * nchunk + j * SUB : a * nchunk + (j + 1) * SUB, :] = term

        def spread_group(j, carry):
            base = pl.multiple_of(j * SUB, SUB)
            row_high = rows_ref[pl.ds(base, SUB), :] // LANES
            terms = [tbuf[pl.ds(a * nchunk + base, SUB), :] for a in range(6)]
            for s in range(SUB):
                here = row_high[s : s + 1, :] - sub_q
                stacked = []
                for p in range(pairs):
                    value = jnp.broadcast_to(terms[p * per][s : s + 1, :], (SUB, LANES))
                    for o in range(1, per):
                        value = jnp.where(sub_b == o, terms[p * per + o][s : s + 1, :], value)
                    stacked.append(value)
                rows = []
                for d in range(nrow):
                    chosen = here == d * qn
                    for p in range(pairs):
                        rows.append(jnp.where(chosen, stacked[p], 0.0))
                full = jnp.concatenate(rows, axis=0)
                upper = full.astype(jnp.bfloat16)
                rest = (full - upper.astype(jnp.float32)).astype(jnp.bfloat16)
                where = pl.ds(pl.multiple_of((j * SUB + s) * LANES, LANES), LANES)
                spread[0 : nrow * vec, where] = upper
                spread[nrow * vec : 2 * nrow * vec, where] = rest
            return carry

        lax.fori_loop(0, nj, spread_group, 0)
        both = lax.dot_general(
            spread[...], onehot[...], (((1,), (1,)), ((), ())),
            preferred_element_type=jnp.float32,
        )
        total = both[: nrow * vec] + both[nrow * vec :]
        for d in range(nrow):
            part[k, d, 0:vec, :] = total[d * vec : (d + 1) * vec]

    def send_parts(k):
        size = msg if k == ITERS - 1 else vec
        copies = []
        for i in range(1, nrow):
            peer = xor_index(my_row, i, nrow)
            copy = pltpu.make_async_remote_copy(
                src_ref=part.at[k, peer, pl.ds(0, size)],
                dst_ref=rbuf.at[k, my_row, pl.ds(0, size)],
                send_sem=ps_sem.at[k, i],
                recv_sem=pr_sem.at[k, i],
                device_id=(peer, my_col),
                device_id_type=MESH,
            )
            copy.start()
            copies.append(copy)
        return copies

    def diag_image(k):
        out = []
        v = [vv[k, b * qn : (b + 1) * qn, :] for b in range(6)]
        for a in range(6):
            value = diag(6 * a) * v[0]
            for b in range(1, 6):
                value = value + diag(6 * a + b) * v[b]
            out.append(value)
        return out

    def row_sum(value):
        return jnp.sum(value, axis=0, keepdims=True)

    moments = [row_sum(vv[0] * rv[0])]
    for k in range(ITERS):
        own = diag_image(k)
        for a in range(6):
            rv[k + 1, a * qn : (a + 1) * qn, :] = rv[k, a * qn : (a + 1) * qn, :] - own[a]
        if k == ITERS - 1:
            curv = row_sum(vv[k] * (rv[k] - rv[k + 1]))
        tile_partial(k)
        if k == ITERS - 1:
            curv = curv + row_sum(vv[k] * part[k, my_row, 0:vec, :])
            for i in range(1, nrow):
                peer = xor_index(my_row, i, nrow)
                row_copies[i - 1].wait_recv()
                curv = curv + row_sum(vrow[peer] * part[k, peer, 0:vec, :])
            moments.append(curv)
            packed = jnp.zeros((SUB, LANES), jnp.float32)
            for n, value in enumerate(moments):
                packed = jnp.where(lane == n, jnp.sum(value, axis=1, keepdims=True), packed)
            for d in range(nrow):
                part[k, d, vec:msg, :] = packed
        sent = send_parts(k)
        image = part[k, my_row, 0:vec, :]
        for i in range(1, nrow):
            sent[i - 1].wait_recv()
            peer = xor_index(my_row, i, nrow)
            image = image + rbuf[k, peer, 0:vec, :]
            if k == ITERS - 1:
                packed = packed + rbuf[k, peer, vec:msg, :]
        sends += sent
        if k == ITERS - 1:
            mown[...] = packed
            total_m = packed
            mom_sends = []
            for i in range(1, ncol):
                copy = pltpu.make_async_remote_copy(
                    src_ref=mown,
                    dst_ref=mom.at[my_col],
                    send_sem=ms_sem.at[i],
                    recv_sem=mr_sem.at[i],
                    device_id=(my_row, xor_index(my_col, i, ncol)),
                    device_id_type=MESH,
                )
                copy.start()
                mom_sends.append(copy)
        rv[k + 1] = rv[k + 1] - image
        if k + 1 < ITERS:
            precondition(k + 1)
            sends += send_vector(k + 1)
            if k + 1 == ITERS - 1:
                row_copies = send_rows(k + 1)
            moments.append(row_sum(vv[k] * rv[k + 1]))
            moments.append(row_sum(vv[k + 1] * rv[k + 1]))

    for i in range(1, ncol):
        mom_sends[i - 1].wait_recv()
        total_m = total_m + mom[xor_index(my_col, i, ncol)]
    m = [
        jnp.broadcast_to(
            jnp.sum(jnp.where(lane == n, total_m, 0.0), axis=1, keepdims=True), (SUB, LANES)
        )
        for n in range(2 * ITERS)
    ]
    m[2 * ITERS - 1] = m[2 * ITERS - 2] - m[2 * ITERS - 1]
    xc, rc = cg_scalars(m)
    for b in range(6):
        for q in range(qn):
            n = b * qn + q
            x = None
            r = None
            for k in range(ITERS + 1):
                add = rc[k][0:1] * rv[k, n : n + 1, :]
                r = add if r is None else r + add
                if k < ITERS:
                    add = xc[k][0:1] * vv[k, n : n + 1, :]
                    x = add if x is None else x + add
            x_ref[b : b + 1, q * LANES : (q + 1) * LANES] = x
            r_ref[b : b + 1, q * LANES : (q + 1) * LANES] = r
    for copy in sends + row_copies + mom_sends:
        copy.wait_send()


def on_device(nrow, ncol, minus_gradient, diag_blocks, hess_blocks, block_rows, block_cols, counts):
    pose_dev = minus_gradient.shape[1]
    nslot = block_rows.shape[-1]
    nchunk = nslot // LANES
    vec = 6 * pose_dev // LANES
    msg = vec + SUB
    f32 = jnp.float32
    vmem = pl.BlockSpec(memory_space=pltpu.VMEM)
    dma = pltpu.SemaphoreType.DMA
    out = jax.ShapeDtypeStruct(minus_gradient.shape, f32)
    return pl.pallas_call(
        functools.partial(kernel, nrow, ncol),
        out_shape=(out, out),
        in_specs=[
            pl.BlockSpec(memory_space=pltpu.SMEM), vmem, vmem, vmem, vmem,
            pl.BlockSpec(memory_space=pl.ANY),
        ],
        out_specs=(vmem, vmem),
        scratch_shapes=[
            pltpu.VMEM((36, nslot), f32),
            pltpu.VMEM((36 * (nchunk + SUB), LANES), f32),
            pltpu.VMEM((6 * vec, LANES), f32),
            pltpu.VMEM((21, pose_dev // LANES, LANES), f32),
            pltpu.VMEM((ITERS + 1, vec, LANES), f32),
            pltpu.VMEM((ITERS, vec, LANES), f32),
            pltpu.VMEM((ITERS, ncol, vec, LANES), f32),
            pltpu.VMEM((nrow, vec, LANES), f32),
            pltpu.VMEM((6 * nchunk, LANES), f32),
            pltpu.VMEM((2 * nrow * vec, nslot), jnp.bfloat16),
            pltpu.VMEM((LANES, nslot), jnp.bfloat16),
            pltpu.VMEM((ITERS, nrow, msg, LANES), f32),
            pltpu.VMEM((ITERS, nrow, msg, LANES), f32),
            pltpu.VMEM((ncol, SUB, LANES), f32),
            pltpu.VMEM((SUB, LANES), f32),
            dma,
            dma((ITERS, ncol)), dma((ITERS, ncol)),
            dma((nrow,)), dma((nrow,)),
            dma((ITERS, nrow)), dma((ITERS, nrow)),
            dma((ncol,)), dma((ncol,)),
        ],
        compiler_params=pltpu.CompilerParams(
            collective_id=0, has_side_effects=True, vmem_limit_bytes=48 * 1024 * 1024
        ),
    )(
        counts,
        minus_gradient,
        diag_blocks,
        block_rows.reshape(nchunk, LANES),
        block_cols.reshape(nchunk, LANES),
        hess_blocks.reshape(36, nslot),
    )


def solution(mesh):
    placed = (
        P(None, ("row", "col")),
        P(None, ("row", "col")),
        P("row", "col", None, None),
        P("row", "col", None),
        P("row", "col", None),
        P("row", "col"),
    )
    return jax.shard_map(
        functools.partial(on_device, mesh.shape["row"], mesh.shape["col"]),
        mesh=mesh,
        in_specs=placed,
        out_specs=(P(None, ("row", "col")), P(None, ("row", "col"))),
        check_vma=False,
    )
```

time: 248 us -> 42.7 us (0.17)
  blocking collectives: 201 us -> 0 us
  Pallas kernels: 0 us -> 38.5 us
  matrix products: 16.6 us -> 0 us
  other arithmetic: 11.1 us -> 0 us
  between operations: 11.5 us -> 1.35 us
  loops' own time: 2.93 us -> 0 us
    psum x6 -> x0, blocking collectives: 170 us -> none  [the longest x3 113 us: merged_sums(): lax.psum((jnp.sum(residual * precond), jnp.sum(hess_image * precond)), ('...]
    pallas_call x0 -> x1, Pallas kernels: none -> 38.5 us  [on_device(): pl.pallas_call(functools.partial(kernel, nrow, ncol), out_shape=(out, out...]
    all_gather x3 -> x0, blocking collectives: 31.1 us -> none  [hessian(): gathered = lax.all_gather(vector, 'col', axis=1, tiled=True)]
    dot_general x48 -> x0, matrix products: 16.6 us -> none  [the longest x24 8.61 us: add_one_block(): jnp.dot(spread, low_onehot, precision=lax.Precision.HIGHEST, preferred_el...]
    reduce_sum x33 -> x0, other arithmetic: 4.13 us -> none  [the longest x3 1.92 us: merged_sums(): jnp.sum(hess_image * precond)]
    another operation x6 -> x0, loops' own time: 2.93 us -> none  [the longest x3 1.49 us: add_rows(): lax.scan(add_one_block, start_total, (term_blocks, row_blocks))]
    unnamed x6 -> x0, other arithmetic: 2.78 us -> none
where the time goes in v1:
time: 42.7 us; the launch traced here: 42.6 us
  Pallas kernels  38.5 us (90%)
  local copies, waits for them, and re-layouts  2.69 us (6%)
  between operations  1.35 us (3%)
    pallas_call x1, Pallas kernels, on_device(): pl.pallas_call(functools.partial(kernel, nrow, ncol), out_shape=(out, out...  38.5 us
    unnamed x11, local copies, waits for them, and re-layouts  2.69 us

profile of v1, /device:TPU:0, one launch (start us, length us, event | category | flops | bytes accessed | tf_op | source)
XLA Modules:
  0.0 42.6 jit_solution(342183745239956360)
XLA Ops:
  1.3 0.0 copy-start
  1.3 0.0 copy-start.1
  1.3 0.0 copy-start.2
  1.3 0.0 copy-start.3
  1.3 1.5 %copy.10 = f32[1,1,36,4096]{3,2,1,0:T(8,128)S(1)} copy(f32[1,1,36,4096]{3,1,2,0:T(1,128)} %param.8) | data formatting | bytes 1179648
  2.8 0.0 copy-done
  2.8 0.0 copy-done.1
  2.8 0.0 copy-done.2
  2.8 0.0 copy-done.3
  2.8 38.5 %shard_map.77 = (f32[6,512]{1,0:T(8,128)S(1)}, f32[6,512]{1,0:T(8,128)S(1)}) custom-call(s32[1,1]{1,0:T(1,128)S(6)} %copy.13.cnt_ref, f32[6,512]{1,0:T(8,128)S(1)} %copy-done.1, f32[36,512]{1,0:T(8,128)S(1)} %copy-done, s32[32,128]{1,0:T(8,128)S(1)} %bitcast.6, s32[32,128]{1,0:T(8,128)S(1)} %bitcast.7, f32[36,4096]{1,0:T(8,128)S(1)} %bitcast.5), custom_call_target="tpu_custom_call" | custom-call | tf_op jit(solution)/shard_map/pallas_call | solution.py:402
  41.4 0.6 %copy.14 = f32[6,512]{1,0:T(8,128)} copy(f32[6,512]{1,0:T(8,128)S(1)} %get-tuple-element.4) | data formatting | bytes 24576
  42.0 0.6 %copy.15 = f32[6,512]{1,0:T(8,128)} copy(f32[6,512]{1,0:T(8,128)S(1)} %get-tuple-element.5) | data formatting | bytes 24576
Async XLA Ops:
  1.3 1.5 %copy-start = (f32[36,512]{1,0:T(8,128)S(1)}, f32[36,512]{1,0:T(8,128)}, u32[]{:S(2)}) copy-start(f32[36,512]{1,0:T(8,128)} %d_ref.1) | copy-start | bytes 221188
  1.3 1.5 %copy-start.1 = (f32[6,512]{1,0:T(8,128)S(1)}, f32[6,512]{1,0:T(8,128)}, u32[]{:S(2)}) copy-start(f32[6,512]{1,0:T(8,128)} %g_ref.1) | copy-start | bytes 36868
  1.3 1.5 %copy-start.2 = (s32[1,1,4096]{2,1,0:T(1,128)S(1)}, s32[1,1,4096]{2,1,0:T(1,128)}, u32[]{:S(2)}) copy-start(s32[1,1,4096]{2,1,0:T(1,128)} %param.9) | copy-start | bytes 49156
  1.3 1.5 %copy-start.3 = (s32[1,1,4096]{2,1,0:T(1,128)S(1)}, s32[1,1,4096]{2,1,0:T(1,128)}, u32[]{:S(2)}) copy-start(s32[1,1,4096]{2,1,0:T(1,128)} %param.10) | copy-start | bytes 49156

commit v2 on v1

--- a/solution.py
+++ b/solution.py
@@ -20,6 +20,12 @@
         out = out + bit * ((a // bit + b // bit) % 2)
         bit *= 2
     return out
+
+
+def split_index(value, size):
+    if size & (size - 1) == 0:
+        return value >> (size.bit_length() - 1), value & (size - 1)
+    return lax.div(value, size), lax.rem(value, size)
 
 
 def factor_blocks(entry):
@@ -84,15 +90,14 @@
 
 
 def kernel(
-    nrow, ncol, cnt_ref, g_ref, d_ref, rows_ref, cols_ref, h_any, x_ref, r_ref,
-    hbuf, b3, dbuf, lbuf, rv, vv, tab, vrow, tbuf, spread, onehot, part, rbuf, mom, mown,
-    hsem, vs_sem, vr_sem, ws_sem, wr_sem, ps_sem, pr_sem, ms_sem, mr_sem,
+    nrow, ncol, cnt_any, g_any, d_any, rows_any, cols_any, h_any, x_ref, r_ref,
+    cnt_ref, g_ref, d_ref, rows_ref, cols_ref, b3, dbuf, lbuf, rv, vv, tab, vrow, key, tbuf, spread, onehot, part, rbuf, mom, mown,
+    in_sem, vs_sem, vr_sem, ws_sem, wr_sem, ps_sem, pr_sem, ms_sem, mr_sem,
 ):
     pose_dev = g_ref.shape[1]
     qn = pose_dev // LANES
     vec = 6 * qn
     nchunk = rows_ref.shape[0]
-    stride = nchunk + SUB
     nj = nchunk // SUB
     msg = part.shape[2]
     per = SUB // qn
@@ -100,8 +105,17 @@
     my_row = lax.axis_index("row")
     my_col = lax.axis_index("col")
 
-    h_copy = pltpu.make_async_copy(h_any, hbuf, hsem)
-    h_copy.start()
+    loads = [
+        pltpu.make_async_copy(source, target, in_sem.at[n])
+        for n, (source, target) in enumerate(
+            [
+                (d_any, d_ref), (g_any, g_ref), (rows_any, rows_ref),
+                (cols_any, cols_ref), (h_any, b3), (cnt_any, cnt_ref),
+            ]
+        )
+    ]
+    for load in loads:
+        load.start()
 
     barrier = pltpu.get_barrier_semaphore()
     for i in range(1, ncol):
@@ -113,6 +127,8 @@
             barrier, inc=1, device_id=(xor_index(my_row, i, nrow), my_col), device_id_type=MESH
         )
 
+    loads[0].wait()
+    loads[1].wait()
     for b in range(6):
         for q in range(qn):
             rv[0, b * qn + q : b * qn + q + 1, :] = g_ref[b : b + 1, q * LANES : (q + 1) * LANES]
@@ -128,8 +144,8 @@
 
     lower_part, reciprocals = factor_blocks(diag)
     slot_of = {}
-    for n, (key, value) in enumerate(list(lower_part.items()) + list(enumerate(reciprocals))):
-        slot_of[key] = n
+    for n, (name, value) in enumerate(list(lower_part.items()) + list(enumerate(reciprocals))):
+        slot_of[name] = n
         lbuf[n] = value
 
     def lower(i, k):
@@ -177,36 +193,38 @@
     pl.semaphore_wait(barrier, ncol + nrow - 2)
     sends = send_vector(0)
 
-    sub_low = lax.broadcasted_iota(jnp.int32, (LANES, LANES), 0)
+    wide = 2 * LANES
+    hot_row = lax.broadcasted_iota(jnp.int32, (wide, LANES), 0)
 
     def build_onehot(j, carry):
-        low = rows_ref[pl.ds(pl.multiple_of(j * SUB, SUB), SUB), :] % LANES
+        row = rows_ref[pl.ds(pl.multiple_of(j * SUB, SUB), SUB), :]
+        chunk, low = split_index(row, LANES)
+        group, q = split_index(chunk, qn)
+        group_half, parity = split_index(group, 2)
+        key[pl.ds(pl.multiple_of(j * SUB, SUB), SUB), :] = group_half * qn + q
+        target = parity * LANES + low
         for s in range(SUB):
-            hot = jnp.where(sub_low == low[s : s + 1, :], 1.0, 0.0).astype(jnp.bfloat16)
+            hot = jnp.where(hot_row == target[s : s + 1, :], 1.0, 0.0).astype(jnp.bfloat16)
             onehot[:, pl.ds(pl.multiple_of((j * SUB + s) * LANES, LANES), LANES)] = hot
         return carry
 
+    loads[2].wait()
     lax.fori_loop(0, nj, build_onehot, 0)
 
-    h_copy.wait()
+    loads[3].wait()
+    loads[4].wait()
+    loads[5].wait()
     live_count = cnt_ref[0, 0]
     lane = lax.broadcasted_iota(jnp.int32, (SUB, LANES), 1)
-    for c in range(nchunk):
-        live = lane + c * LANES < live_count
-        for e in range(0, 36, SUB):
-            count = min(SUB, 36 - e)
-            tile = hbuf[e : e + count, c * LANES : (c + 1) * LANES]
-            b3[pl.ds(e * stride + c, count, stride=stride), :] = jnp.where(
-                live[:count], tile, 0.0
-            )
-
     sub = lax.broadcasted_iota(jnp.int32, (SUB, LANES), 0)
     sub_q = sub % qn
     sub_b = sub // qn
+    slot_id = sub * LANES + lane
 
     def tile_partial(k):
-        low = [cols_ref[j * SUB : (j + 1) * SUB, :] % LANES for j in range(nj)]
-        high = [cols_ref[j * SUB : (j + 1) * SUB, :] // LANES for j in range(nj)]
+        split = [split_index(cols_ref[j * SUB : (j + 1) * SUB, :], LANES) for j in range(nj)]
+        high = [pair[0] for pair in split]
+        low = [pair[1] for pair in split]
 
         def pick(dev, source, acc):
             acc = list(acc)
@@ -235,48 +253,48 @@
             return pick(peer, lambda n: tab[k, peer, n : n + 1, :], acc)
 
         acc = lax.fori_loop(1, ncol, one_peer, acc)
-        for a in range(6):
-            for j in range(nj):
+        halves = nrow // 2
+        both = None
+        for j in range(nj):
+            for a in range(6):
                 term = None
                 for b in range(6):
-                    start = (6 * a + b) * stride + j * SUB
-                    product = b3[start : start + SUB, :] * acc[b * nj + j]
+                    product = b3[6 * a + b, j * SUB : (j + 1) * SUB, :] * acc[b * nj + j]
                     term = product if term is None else term + product
-                tbuf[a * nchunk + j * SUB : a * nchunk + (j + 1) * SUB, :] = term
-
-        def spread_group(j, carry):
-            base = pl.multiple_of(j * SUB, SUB)
-            row_high = rows_ref[pl.ds(base, SUB), :] // LANES
-            terms = [tbuf[pl.ds(a * nchunk + base, SUB), :] for a in range(6)]
-            for s in range(SUB):
-                here = row_high[s : s + 1, :] - sub_q
+                tbuf[a * nchunk + j * SUB : a * nchunk + (j + 1) * SUB, :] = jnp.where(
+                    slot_id + j * SUB * LANES < live_count, term, 0.0
+                )
+            for c in range(j * SUB, (j + 1) * SUB):
+                here = jnp.broadcast_to(key[c : c + 1, :], (SUB, LANES)) - sub_q
                 stacked = []
                 for p in range(pairs):
-                    value = jnp.broadcast_to(terms[p * per][s : s + 1, :], (SUB, LANES))
+                    first = p * per * nchunk + c
+                    value = jnp.broadcast_to(tbuf[first : first + 1, :], (SUB, LANES))
                     for o in range(1, per):
-                        value = jnp.where(sub_b == o, terms[p * per + o][s : s + 1, :], value)
+                        n = (p * per + o) * nchunk + c
+                        other = jnp.broadcast_to(tbuf[n : n + 1, :], (SUB, LANES))
+                        value = jnp.where(sub_b == o, other, value)
                     stacked.append(value)
                 rows = []
-                for d in range(nrow):
+                for d in range(halves):
                     chosen = here == d * qn
                     for p in range(pairs):
                         rows.append(jnp.where(chosen, stacked[p], 0.0))
                 full = jnp.concatenate(rows, axis=0)
                 upper = full.astype(jnp.bfloat16)
                 rest = (full - upper.astype(jnp.float32)).astype(jnp.bfloat16)
-                where = pl.ds(pl.multiple_of((j * SUB + s) * LANES, LANES), LANES)
-                spread[0 : nrow * vec, where] = upper
-                spread[nrow * vec : 2 * nrow * vec, where] = rest
-            return carry
-
-        lax.fori_loop(0, nj, spread_group, 0)
-        both = lax.dot_general(
-            spread[...], onehot[...], (((1,), (1,)), ((), ())),
-            preferred_element_type=jnp.float32,
-        )
-        total = both[: nrow * vec] + both[nrow * vec :]
+                spread[0 : halves * vec, c * LANES : (c + 1) * LANES] = upper
+                spread[halves * vec : 2 * halves * vec, c * LANES : (c + 1) * LANES] = rest
+            span = slice(j * SUB * LANES, (j + 1) * SUB * LANES)
+            product = lax.dot_general(
+                spread[:, span], onehot[:, span], (((1,), (1,)), ((), ())),
+                preferred_element_type=jnp.float32,
+            )
+            both = product if both is None else both + product
+        total = both[: halves * vec] + both[halves * vec :]
         for d in range(nrow):
-            part[k, d, 0:vec, :] = total[d * vec : (d + 1) * vec]
+            h, o = d // 2, d % 2
+            part[k, d, 0:vec, :] = total[h * vec : (h + 1) * vec, o * LANES : (o + 1) * LANES]
 
     def send_parts(k):
         size = msg if k == ITERS - 1 else vec
@@ -314,7 +332,9 @@
         for a in range(6):
             rv[k + 1, a * qn : (a + 1) * qn, :] = rv[k, a * qn : (a + 1) * qn, :] - own[a]
         if k == ITERS - 1:
-            curv = row_sum(vv[k] * (rv[k] - rv[k + 1]))
+            curv = 0.0
+            for a in range(6):
+                curv = curv + row_sum(vv[k, a * qn : (a + 1) * qn, :] * own[a])
         tile_partial(k)
         if k == ITERS - 1:
             curv = curv + row_sum(vv[k] * part[k, my_row, 0:vec, :])
@@ -325,7 +345,7 @@
             moments.append(curv)
             packed = jnp.zeros((SUB, LANES), jnp.float32)
             for n, value in enumerate(moments):
-                packed = jnp.where(lane == n, jnp.sum(value, axis=1, keepdims=True), packed)
+                packed = jnp.where(sub == n, jnp.sum(value, axis=1, keepdims=True), packed)
             for d in range(nrow):
                 part[k, d, vec:msg, :] = packed
         sent = send_parts(k)
@@ -364,12 +384,7 @@
     for i in range(1, ncol):
         mom_sends[i - 1].wait_recv()
         total_m = total_m + mom[xor_index(my_col, i, ncol)]
-    m = [
-        jnp.broadcast_to(
-            jnp.sum(jnp.where(lane == n, total_m, 0.0), axis=1, keepdims=True), (SUB, LANES)
-        )
-        for n in range(2 * ITERS)
-    ]
+    m = [total_m[n : n + 1, :] for n in range(2 * ITERS)]
     m[2 * ITERS - 1] = m[2 * ITERS - 2] - m[2 * ITERS - 1]
     xc, rc = cg_scalars(m)
     for b in range(6):
@@ -378,10 +393,10 @@
             x = None
             r = None
             for k in range(ITERS + 1):
-                add = rc[k][0:1] * rv[k, n : n + 1, :]
+                add = rc[k] * rv[k, n : n + 1, :]
                 r = add if r is None else r + add
                 if k < ITERS:
-                    add = xc[k][0:1] * vv[k, n : n + 1, :]
+                    add = xc[k] * vv[k, n : n + 1, :]
                     x = add if x is None else x + add
             x_ref[b : b + 1, q * LANES : (q + 1) * LANES] = x
             r_ref[b : b + 1, q * LANES : (q + 1) * LANES] = r
@@ -403,34 +418,38 @@
         functools.partial(kernel, nrow, ncol),
         out_shape=(out, out),
         in_specs=[
-            pl.BlockSpec(memory_space=pltpu.SMEM), vmem, vmem, vmem, vmem,
-            pl.BlockSpec(memory_space=pl.ANY),
+            pl.BlockSpec(memory_space=pltpu.HBM) for _ in range(6)
         ],
         out_specs=(vmem, vmem),
         scratch_shapes=[
-            pltpu.VMEM((36, nslot), f32),
-            pltpu.VMEM((36 * (nchunk + SUB), LANES), f32),
+            pltpu.SMEM((1, 1), jnp.int32),
+            pltpu.VMEM(minus_gradient.shape, f32),
+            pltpu.VMEM(diag_blocks.shape, f32),
+            pltpu.VMEM((nchunk, LANES), jnp.int32),
+            pltpu.VMEM((nchunk, LANES), jnp.int32),
+            pltpu.VMEM((36, nchunk, LANES), f32),
             pltpu.VMEM((6 * vec, LANES), f32),
             pltpu.VMEM((21, pose_dev // LANES, LANES), f32),
             pltpu.VMEM((ITERS + 1, vec, LANES), f32),
             pltpu.VMEM((ITERS, vec, LANES), f32),
             pltpu.VMEM((ITERS, ncol, vec, LANES), f32),
             pltpu.VMEM((nrow, vec, LANES), f32),
+            pltpu.VMEM((nchunk, LANES), jnp.int32),
             pltpu.VMEM((6 * nchunk, LANES), f32),
-            pltpu.VMEM((2 * nrow * vec, nslot), jnp.bfloat16),
-            pltpu.VMEM((LANES, nslot), jnp.bfloat16),
+            pltpu.VMEM((nrow * vec, nslot), jnp.bfloat16),
+            pltpu.VMEM((2 * LANES, nslot), jnp.bfloat16),
             pltpu.VMEM((ITERS, nrow, msg, LANES), f32),
             pltpu.VMEM((ITERS, nrow, msg, LANES), f32),
             pltpu.VMEM((ncol, SUB, LANES), f32),
             pltpu.VMEM((SUB, LANES), f32),
-            dma,
+            dma((6,)),
             dma((ITERS, ncol)), dma((ITERS, ncol)),
             dma((nrow,)), dma((nrow,)),
             dma((ITERS, nrow)), dma((ITERS, nrow)),
             dma((ncol,)), dma((ncol,)),
         ],
         compiler_params=pltpu.CompilerParams(
-            collective_id=0, has_side_effects=True, vmem_limit_bytes=48 * 1024 * 1024
+            collective_id=0, has_side_effects=True, vmem_limit_bytes=67043328 - 64 * 1024
         ),
     )(
         counts,
@@ -438,7 +457,7 @@
         diag_blocks,
         block_rows.reshape(nchunk, LANES),
         block_cols.reshape(nchunk, LANES),
-        hess_blocks.reshape(36, nslot),
+        hess_blocks.reshape(36, nchunk, LANES),
     )
 
 

time: 42.7 us -> 41.3 us (0.967)
  local copies, waits for them, and re-layouts: 2.69 us -> 1.94 us
  Pallas kernels: 38.5 us -> 37.8 us
    unnamed x11 -> x4, local copies, waits for them, and re-layouts: 2.69 us -> 1.94 us
    pallas_call x1, Pallas kernels: 38.5 us -> 37.8 us  [on_device(): pl.pallas_call(functools.partial(kernel, nrow, ncol), out_shape=(out, out...]
where the time goes in v2:
time: 41.3 us; the launch traced here: 41.1 us
  Pallas kernels  37.8 us (92%)
  local copies, waits for them, and re-layouts  1.94 us (5%)
  between operations  1.3 us (3%)
    pallas_call x1, Pallas kernels, on_device(): pl.pallas_call(functools.partial(kernel, nrow, ncol), out_shape=(out, out...  37.8 us
    unnamed x4, local copies, waits for them, and re-layouts  1.94 us

profile of v2, /device:TPU:0, one launch (start us, length us, event | category | flops | bytes accessed | tf_op | source)
XLA Modules:
  0.0 41.1 jit_solution(13348028109957779011)
XLA Ops:
  1.3 37.8 %shard_map.77 = (f32[6,512]{1,0:T(8,128)}, f32[6,512]{1,0:T(8,128)}) custom-call(s32[1,1]{1,0:T(1,128)S(6)} %copy.10.cnt_any, f32[6,512]{1,0:T(8,128)} %g_any.1, f32[36,512]{1,0:T(8,128)} %d_any.1, s32[32,128]{1,0:T(8,128)} %bitcast.4, s32[32,128]{1,0:T(8,128)} %bitcast.5, f32[36,32,128]{2,1,0:T(8,128)} %bitcast.3), custom_call_target="tpu_custom_call" | custom-call | tf_op jit(solution)/shard_map/pallas_call | solution.py:417
  39.1 0.0 copy-start
  39.1 1.3 %copy.11 = f32[6,512]{1,0:T(8,128)} copy(f32[6,512]{1,0:T(8,128)} %get-tuple-element.4) | data formatting | bytes 24576
  40.5 0.0 copy-done
  40.5 0.6 %copy.12 = f32[6,512]{1,0:T(8,128)} copy(f32[6,512]{1,0:T(8,128)S(1)} %copy-done) | data formatting | bytes 24576
Async XLA Ops:
  39.1 1.3 %copy-start = (f32[6,512]{1,0:T(8,128)S(1)}, f32[6,512]{1,0:T(8,128)}, u32[]{:S(2)}) copy-start(f32[6,512]{1,0:T(8,128)} %get-tuple-element.5) | copy-start | bytes 36868
